TPU v7x, 32 devices: a whole 2x2x4 slice. The times are simulated.
32 devices in a mesh: prow: 4 (over z), pcol: 8 (over y, x, core).
Axes of the slice: x: 2, y: 2, z: 4, core: 2. Of those that a mesh axis runs over, the one named last changes fastest.
Arguments:
- points: float32 [1, 8, 2, 1024], P(None, 'pcol'), may hold values from 0 to 1
- range_length: float32 [1], replicated, may hold values from 0.05 to 0.15
- smoothness: int32 [1], replicated, may hold values from 0 to 2
- sketch_bank: bfloat16 [8, 48, 1024], P('pcol'), may hold values from -6 to 6
- sketch_ids: int32 [2, 4, 1, 8], P(None, 'prow', None, 'pcol'), may hold values from 0 to 7
- tile_ranks: int32 [2, 4, 1, 8], P(None, 'prow', None, 'pcol'), may hold values from 16 to 48
Outputs:
- y_factors: float32 [2, 4, 1, 8, 48, 1024], P(None, 'prow', None, 'pcol')
- c_factors: float32 [2, 4, 1, 8, 48, 1024], P(None, 'prow', None, 'pcol')
- tile_error: float32 [2, 4, 1, 8], P(None, 'prow', None, 'pcol')
- rank_total: int32 [1], replicated
All inputs are finite; a program needn't handle non-finite values.
Results may differ from a plain program's by a relative error of at most 0.0098.
The roundings to bfloat16 on the way count: a program that leaves them out, or rounds other values in their place, can miss the bound.
Values may be sent and summed in bfloat16 or wider, within the bound.
A program may use at most 64 MiB of HBM per device.

v0:
```python
import functools
import math

import jax
import jax.numpy as jnp
from jax import lax
from jax.experimental import pallas as pl
from jax.experimental.pallas import tpu as pltpu
from jax.sharding import PartitionSpec as P

MESH = pl.DeviceIdType.MESH
LOG2E = math.log2(math.e)
F32 = jnp.float32
BF16 = jnp.bfloat16
HIGH = lax.Precision.HIGHEST


def dot(a, b, da, db, precision=None):
    return lax.dot_general(
        a, b, (((da,), (db,)), ((), ())), preferred_element_type=F32, precision=precision
    )


def split(x):
    high = x.astype(BF16)
    return high, (x - high.astype(F32)).astype(BF16)


def all_sum(x):
    return jnp.sum(jnp.sum(x, axis=1, keepdims=True), axis=0, keepdims=True)


def invert(mats, group=8):
    size = mats[0].shape[0]
    parts = size // 8
    sub = lax.broadcasted_iota(jnp.int32, (8, size), 0)
    lane = lax.broadcasted_iota(jnp.int32, (8, size), 1)
    mats = [[m[8 * v : 8 * v + 8] for v in range(parts)] for m in mats]
    for start in range(0, size, group):
        spread = [
            {
                k: [jnp.broadcast_to(part[:, k : k + 1], (8, size)) for part in m]
                for k in range(start, start + group)
            }
            for m in mats
        ]
        for k in range(start, start + group):
            at, within = divmod(k, 8)
            for index, (m, cols) in enumerate(zip(mats, spread)):
                col = cols.pop(k)
                pivot = jnp.broadcast_to(col[at][within : within + 1], (8, size))
                inverse = 1.0 / pivot
                for other, entry in cols.items():
                    head = jnp.broadcast_to(entry[at][within : within + 1], (8, size)) * inverse
                    entry = [e - c * head for e, c in zip(entry, col)]
                    entry[at] = jnp.where(sub == within, head, entry[at])
                    cols[other] = entry
                row = jnp.broadcast_to(m[at][within : within + 1], (8, size))
                row = jnp.where(lane == k, 1.0, row) * inverse
                m = [jnp.where(lane == k, 0.0, part) - c * row for part, c in zip(m, col)]
                m[at] = jnp.where(sub == within, row, m[at])
                mats[index] = m
    return [jnp.concatenate(m, axis=0) for m in mats]


def kernel(
    rows,
    cols,
    row_tiles,
    col_tiles,
    range_length,
    smoothness,
    points_hbm,
    bank_hbm,
    ids_hbm,
    ranks_hbm,
    y_out,
    c_out,
    residuals,
    whole_out,
    points,
    ids,
    ranks,
    all_points,
    all_bank,
    low,
    norms,
    mine,
    sums,
    sem_local,
    sem_ps,
    sem_pr,
    sem_bs,
    sem_br,
    sem_ns,
    sem_nr,
    ready,
):
    p = lax.axis_index("prow")
    q = lax.axis_index("pcol")
    per_bank, sketch_rows, size = bank_hbm.shape
    slots = [(a, b) for a in range(row_tiles) for b in range(col_tiles)]
    sibling = q + 1 - 2 * lax.rem(q, 2)

    barrier = pltpu.get_barrier_semaphore()
    for step in range(1, cols):
        pl.semaphore_signal(
            barrier, device_id=(p, lax.rem(q + step, cols)), device_id_type=MESH
        )
    for step in range(1, rows):
        pl.semaphore_signal(
            barrier, device_id=(lax.rem(p + step, rows), q), device_id_type=MESH
        )
    local = [
        pltpu.make_async_copy(source, target, sem_local.at[index])
        for index, (source, target) in enumerate(
            [
                (points_hbm, points),
                (ids_hbm, ids),
                (ranks_hbm, ranks),
                (points_hbm.at[:, 0], all_points.at[q]),
                (bank_hbm, all_bank.at[pl.ds(q * per_bank, per_bank)]),
            ]
        )
    ]
    for copy in local:
        copy.start()
    needed = q < 0
    for a in range(row_tiles):
        needed = needed | (lax.rem(a * rows + p, cols) == q)
    pl.semaphore_wait(barrier, cols + rows - 2)
    for step in range(1, rows):
        pl.semaphore_signal(
            ready, device_id=(lax.rem(p + step, rows), q), device_id_type=MESH
        )

    def point_copy(source, target):
        return pltpu.make_async_remote_copy(
            src_ref=points_hbm.at[:, 0],
            dst_ref=all_points.at[source],
            send_sem=sem_ps.at[target],
            recv_sem=sem_pr.at[source],
            device_id=(p, target),
            device_id_type=MESH,
        )

    def bank_copy(block, target, send):
        return pltpu.make_async_remote_copy(
            src_ref=all_bank.at[pl.ds(block * per_bank, per_bank)] if send >= cols else bank_hbm,
            dst_ref=all_bank.at[pl.ds(block * per_bank, per_bank)],
            send_sem=sem_bs.at[send],
            recv_sem=sem_br.at[block],
            device_id=(p, target),
            device_id_type=MESH,
        )

    @pl.when(needed)
    def _():
        for step in range(1, cols):
            point_copy(q, lax.rem(q + step, cols)).start()

    for step in range(2, cols, 2):
        bank_copy(q, lax.rem(q + step, cols), step).start()
    bank_copy(q, sibling, 1).start()

    for copy in local[:-1]:
        copy.wait()
    degree = jnp.full((8, 128), smoothness[0].astype(F32))
    scale = (LOG2E * jnp.sqrt(2.0 * degree + 1.0)) / jnp.full((8, 128), range_length[0])
    scale = scale[:1]
    linear = jnp.where(smoothness[0] >= 1, 1.0 / LOG2E, 0.0).astype(F32)
    square = jnp.where(smoothness[0] >= 2, 1.0 / (3.0 * LOG2E * LOG2E), 0.0).astype(F32)

    def place(slot):
        a, b = slots[slot]
        return a * rows + p, b * cols + q

    arrived = []

    def generate(slot, begin=0, end=size // 128):
        i, j = place(slot)
        a = slots[slot][0]
        owner = lax.rem(a * rows + p, cols)
        fresh = owner != q
        for before in arrived:
            if before != a:
                fresh = fresh & (owner != lax.rem(before * rows + p, cols))
        if a not in arrived and begin == 0:
            arrived.append(a)

            @pl.when(fresh)
            def _():
                point_copy(owner, q).wait_recv()

        @pl.when(j > i)
        def _():
            norms[slot] = jnp.zeros((8, 128), F32)

        @pl.when(j <= i)
        def _():
            row_block = lax.rem(i, cols)
            row_major = i // cols
            col_major = slots[slot][1]

            def chunk(c, total):
                at = pl.ds(pl.multiple_of(c * 128, 128), 128)
                x_row = all_points[row_block, row_major, 0:1, at] * scale
                y_row = all_points[row_block, row_major, 1:2, at] * scale
                x_row = jnp.broadcast_to(x_row, (128, 128)).T
                y_row = jnp.broadcast_to(y_row, (128, 128)).T
                for n in range(size // 128):
                    cut = slice(n * 128, n * 128 + 128)
                    x_col = points[col_major, 0, 0:1, cut] * scale
                    y_col = points[col_major, 0, 1:2, cut] * scale
                    dx = x_row - x_col
                    dy = y_row - y_col
                    d2 = dx * dx + dy * dy
                    t = d2 * lax.rsqrt(jnp.maximum(d2, 1e-30))
                    tile = (1.0 + linear * t + square * d2) * jnp.exp2(-t)
                    low[slot, at, cut] = tile.astype(BF16)
                    total = total + jnp.sum((tile * tile).reshape(16, 8, 128), axis=0)
                return total

            total = jnp.zeros((8, 128), F32) if begin == 0 else norms[slot]
            norms[slot] = lax.fori_loop(begin, end, chunk, total)

    def forward(steps):
        for step in steps:
            block = lax.rem(q + step, cols)
            bank_copy(block, q, 0).wait_recv()
            bank_copy(block, sibling, cols + step).start()

    for slot in range(len(slots) - 1):
        generate(slot)
    half = size // 256
    generate(len(slots) - 1, 0, half)
    forward(range(2, cols, 2))
    generate(len(slots) - 1, half)

    devices = rows * cols
    me = p * cols + q

    def norm_copy(source, target):
        return pltpu.make_async_remote_copy(
            src_ref=mine,
            dst_ref=sums.at[source],
            send_sem=sem_ns.at[target],
            recv_sem=sem_nr.at[source],
            device_id=(target // cols, lax.rem(target, cols)),
            device_id_type=MESH,
        )

    norm_sum = jnp.zeros((8, 128), F32)
    rank_sum = jnp.float32(0)
    for slot, (a, b) in enumerate(slots):
        i, j = place(slot)
        norm_sum = norm_sum + jnp.where(j < i, 2.0, 1.0).astype(F32) * norms[slot]
        rank_sum = rank_sum + jnp.where(j < i, ranks[0, b, 0, a], 0).astype(F32)
    mine[0:1, :] = jnp.sum(norm_sum, axis=0, keepdims=True)
    mine[1:2, :] = jnp.full((1, 128), rank_sum)

    pl.semaphore_wait(ready, rows - 1)
    for step in range(1, devices):
        norm_copy(me, lax.rem(me + step, devices)).start()

    local[-1].wait()
    bank_copy(sibling, q, 0).wait_recv()
    for step in range(2, cols, 2):
        bank_copy(lax.rem(sibling + step, cols), q, 0).wait_recv()

    def keep_of(a, b):
        return lax.broadcasted_iota(jnp.int32, (sketch_rows, 1), 0) < ranks[0, b, 0, a]

    for slot, (a, b) in enumerate(slots):
        i, j = place(slot)

        @pl.when(j < i)
        def _():
            sketch = all_bank[ids[0, b, 0, a]]
            sketch = jnp.where(keep_of(a, b), sketch.astype(F32), 0.0).astype(BF16)
            y_out[a, 0, b, 0] = dot(sketch, low[slot], 1, 1)

        @pl.when(j >= i)
        def _():
            y_out[a, 0, b, 0] = jnp.zeros((sketch_rows, size), F32)
            c_out[a, 0, b, 0] = jnp.zeros((sketch_rows, size), F32)
            residuals[slot] = norms[slot]

    eye = lax.broadcasted_iota(jnp.int32, (sketch_rows, sketch_rows), 0) == (
        lax.broadcasted_iota(jnp.int32, (sketch_rows, sketch_rows), 1)
    )
    grams = []
    for slot, (a, b) in enumerate(slots):
        i, j = place(slot)
        y = y_out[a, 0, b, 0]
        gram = dot(y, y, 1, 1, HIGH)
        rank = jnp.full((1, 1), ranks[0, b, 0, a].astype(F32))
        shift = 0.1 * all_sum(jnp.where(eye, gram, 0.0)) / rank
        diagonal = jnp.where(keep_of(a, b) & (j < i), shift, 1.0)
        grams.append(gram + jnp.where(eye, diagonal, 0.0))
    inverses = invert(grams)

    for slot, (a, b) in enumerate(slots):
        i, j = place(slot)

        @pl.when(j < i)
        def _():
            product = dot(y_out[a, 0, b, 0].astype(BF16), low[slot], 1, 0)
            c_out[a, 0, b, 0] = dot(inverses[slot], product, 1, 0, HIGH)

    for slot, (a, b) in enumerate(slots):
        i, j = place(slot)

        @pl.when(j < i)
        def _():
            y_high, y_low = split(y_out[a, 0, b, 0])
            c_high, c_low = split(c_out[a, 0, b, 0])
            left = jnp.concatenate([y_high, y_high, y_low], axis=0)
            right = jnp.concatenate([c_high, c_low, c_high], axis=0)
            total = jnp.zeros((8, 128), F32)
            for m in range(size // 128):
                cut = slice(m * 128, m * 128 + 128)
                gap = low[slot, cut].astype(F32) - dot(left[:, cut], right, 0, 0)
                gap = gap * gap
                for n in range(size // 128):
                    total = total + jnp.sum(
                        gap[:, n * 128 : n * 128 + 128].reshape(16, 8, 128), axis=0
                    )
            residuals[slot] = total

    whole = mine[...]
    for step in range(1, devices):
        source = lax.rem(me + step, devices)
        norm_copy(source, me).wait_recv()
        whole = whole + sums[source]
    whole_out[...] = whole

    for step in range(1, devices):
        norm_copy(me, lax.rem(me + step, devices)).wait_send()

    @pl.when(needed)
    def _():
        for step in range(1, cols):
            point_copy(q, lax.rem(q + step, cols)).wait_send()

    for step in range(2, cols, 2):
        bank_copy(q, lax.rem(q + step, cols), step).wait_send()
        bank_copy(lax.rem(q + step, cols), sibling, cols + step).wait_send()
    bank_copy(q, sibling, 1).wait_send()


def finish(rows, cols, row_tiles, col_tiles, y, c, residuals, whole, y_out, c_out, err_out, rank_out, sems):
    p = lax.axis_index("prow")
    q = lax.axis_index("pcol")
    copies = [
        pltpu.make_async_copy(source.at[a], target.at[a], sems.at[index, a])
        for index, (source, target) in enumerate([(y, y_out), (c, c_out)])
        for a in range(row_tiles)
    ]
    for copy in copies:
        copy.start()
    norm = lax.rsqrt(all_sum(whole[0:1, :])) * float(cols * col_tiles)
    lane = lax.broadcasted_iota(jnp.int32, (1, 128), 1)
    for b in range(col_tiles):
        line = jnp.zeros((1, 128), F32)
        for a in range(row_tiles):
            error = jnp.sqrt(all_sum(residuals[a * col_tiles + b])) * norm
            shown = (lane == a) & (b * cols + q <= a * rows + p)
            line = jnp.where(shown, error, line)
        err_out[0, b, 0:1, :] = line[:, :row_tiles]
    rank_out[0] = whole[1:2, 0:1].astype(jnp.int32)[0, 0]
    for copy in copies:
        copy.wait()


def per_device(rows, cols, points, range_length, smoothness, bank, ids, ranks):
    row_tiles, col_tiles = ids.shape[0], ids.shape[2]
    per_bank, sketch_rows, size = bank.shape
    slots = row_tiles * col_tiles
    ids = ids.transpose(1, 2, 3, 0)
    ranks = ranks.transpose(1, 2, 3, 0)
    factors = jax.ShapeDtypeStruct((row_tiles, 1, col_tiles, 1, sketch_rows, size), F32)
    vmem = pl.BlockSpec(memory_space=pltpu.VMEM)
    smem = pl.BlockSpec(memory_space=pltpu.SMEM)
    hbm = pl.BlockSpec(memory_space=pltpu.HBM)
    dma = pltpu.SemaphoreType.DMA
    pinned = [pltpu.with_memory_space_constraint(x, pltpu.HBM) for x in (points, bank, ids, ranks)]
    y, c, residuals, whole = pl.pallas_call(
        functools.partial(kernel, rows, cols, row_tiles, col_tiles),
        out_shape=(
            factors,
            factors,
            jax.ShapeDtypeStruct((slots, 8, 128), F32),
            jax.ShapeDtypeStruct((2, 128), F32),
        ),
        in_specs=[smem, smem, hbm, hbm, hbm, hbm],
        out_specs=(vmem,) * 4,
        scratch_shapes=[
            pltpu.VMEM(points.shape, F32),
            pltpu.SMEM(ids.shape, jnp.int32),
            pltpu.SMEM(ranks.shape, jnp.int32),
            pltpu.VMEM((cols, col_tiles, 2, size), F32),
            pltpu.VMEM((cols * per_bank, sketch_rows, size), BF16),
            pltpu.VMEM((slots, size, size), BF16),
            pltpu.VMEM((slots, 8, 128), F32),
            pltpu.VMEM((2, 128), F32),
            pltpu.VMEM((rows * cols, 2, 128), F32),
            dma((5,)),
            dma((cols,)),
            dma((cols,)),
            dma((2 * cols,)),
            dma((cols,)),
            dma((rows * cols,)),
            dma((rows * cols,)),
            pltpu.SemaphoreType.REGULAR,
        ],
        compiler_params=pltpu.CompilerParams(
            collective_id=0, has_side_effects=True, vmem_limit_bytes=40 * 1024 * 1024
        ),
        name="tiles",
    )(range_length, smoothness, *pinned)
    y, c, errors, rank_total = pl.pallas_call(
        functools.partial(finish, rows, cols, row_tiles, col_tiles),
        out_shape=(
            factors,
            factors,
            jax.ShapeDtypeStruct((1, col_tiles, 1, row_tiles), F32),
            jax.ShapeDtypeStruct((1,), jnp.int32),
        ),
        in_specs=[vmem] * 4,
        out_specs=(hbm, hbm, vmem, smem),
        scratch_shapes=[dma((2, row_tiles))],
        compiler_params=pltpu.CompilerParams(vmem_limit_bytes=16 * 1024 * 1024),
        name="finish",
    )(y, c, residuals, whole)
    return y, c, errors.transpose(3, 0, 1, 2), rank_total


def solution(mesh):
    in_specs = (
        P(None, "pcol", None, None),
        P(),
        P(),
        P("pcol", None, None),
        P(None, "prow", None, "pcol"),
        P(None, "prow", None, "pcol"),
    )
    out_specs = (
        P(None, "prow", None, "pcol", None, None),
        P(None, "prow", None, "pcol", None, None),
        P(None, "prow", None, "pcol"),
        P(),
    )
    return jax.shard_map(
        functools.partial(per_device, mesh.shape["prow"], mesh.shape["pcol"]),
        mesh=mesh,
        in_specs=in_specs,
        out_specs=out_specs,
        check_vma=False,
    )
```

profile of v0, /device:TPU:17, one launch (start us, length us, event | category | flops | bytes accessed | tf_op | source)
XLA Modules:
  0.0 23.9 jit_solution(14409768328711052289)
XLA Ops:
  1.9 20.5 %tiles.1 = (f32[2,1,1,1,48,1024]{5,4,3,2,1,0:T(8,128)S(1)}, f32[2,1,1,1,48,1024]{5,4,3,2,1,0:T(8,128)S(1)}, f32[2,8,128]{2,1,0:T(8,128)S(1)}, f32[2,128]{1,0:T(2,128)S(1)}) custom-call(f32[1]{0:T(128)S(6)} %copy.10.range_length, s32[1]{0:T(128)S(6)} %copy.11.smoothness, f32[1,1,2,1024]{3,2,1,0:T(2,128)} %points_hbm.1, bf16[1,48,1024]{2,1,0:T(8,128)(2,1)} %bank_hbm.1, ...), custom_call_target="tpu_custom_call" | custom-call | tf_op jit(solution)/shard_map/tiles/pallas_call | solution.py:388
  22.4 1.4 %finish.1 = (f32[2,1,1,1,48,1024]{5,4,3,2,1,0:T(8,128)}, f32[2,1,1,1,48,1024]{5,4,3,2,1,0:T(8,128)}, f32[1,1,1,2]{3,2,1,0:T(1,128)}, s32[1]{0:T(128)}) custom-call(f32[2,1,1,1,48,1024]{5,4,3,2,1,0:T(8,128)S(1)} %get-tuple-element.12.y, f32[2,1,1,1,48,1024]{5,4,3,2,1,0:T(8,128)S(1)} %get-tuple-element.13.c, f32[2,8,128]{2,1,0:T(8,128)S(1)} %get-tuple-element.14.residuals, ...), custom_call_target="tpu_custom_call" | custom-call | tf_op jit(solution)/shard_map/finish/pallas_call | solution.py:422
where the time goes:
time: 24 us; the launch traced here: 23.9 us
  Pallas kernels  21.9 us (91%)
  between operations  1.93 us (8%)
    pallas_call x1, Pallas kernels, per_device(): pl.pallas_call(functools.partial(kernel, rows, cols, row_tiles, col_tiles...  20.5 us
    pallas_call x1, Pallas kernels, per_device(): pl.pallas_call(functools.partial(finish, rows, cols, row_tiles, col_tiles...  1.43 us

commit v1 on v0

v1 whole, which is shorter than its diff:
```python
import functools
import math

import jax
import jax.numpy as jnp
from jax import lax
from jax.experimental import pallas as pl
from jax.experimental.pallas import tpu as pltpu
from jax.sharding import PartitionSpec as P

MESH = pl.DeviceIdType.MESH
LOG2E = math.log2(math.e)
F32 = jnp.float32
BF16 = jnp.bfloat16
HIGH = lax.Precision.HIGHEST


def dot(a, b, da, db, precision=None):
    return lax.dot_general(
        a, b, (((da,), (db,)), ((), ())), preferred_element_type=F32, precision=precision
    )


def split(x):
    high = x.astype(BF16)
    return high, (x - high.astype(F32)).astype(BF16)


def all_sum(x):
    return jnp.sum(jnp.sum(x, axis=1, keepdims=True), axis=0, keepdims=True)


def invert(m, size, half, group=8):
    parts = size // 8
    width = m.shape[1]
    sub = lax.broadcasted_iota(jnp.int32, (8, width), 0)
    lane = lax.broadcasted_iota(jnp.int32, (8, width), 1)
    side = lane // half * half
    lane = lane - side
    m = [m[8 * v : 8 * v + 8] for v in range(parts)]
    for start in range(0, size, group):
        cols = {
            k: [jnp.take_along_axis(part, side + k, axis=1) for part in m]
            for k in range(start, start + group)
        }
        for k in range(start, start + group):
            at, within = divmod(k, 8)
            col = cols.pop(k)
            pivot = jnp.broadcast_to(col[at][within : within + 1], (8, width))
            inverse = 1.0 / pivot
            for other, entry in cols.items():
                head = jnp.broadcast_to(entry[at][within : within + 1], (8, width)) * inverse
                entry = [e - c * head for e, c in zip(entry, col)]
                entry[at] = jnp.where(sub == within, head, entry[at])
                cols[other] = entry
            row = jnp.broadcast_to(m[at][within : within + 1], (8, width))
            row = jnp.where(lane == k, 1.0, row) * inverse
            m = [jnp.where(lane == k, 0.0, part) - c * row for part, c in zip(m, col)]
            m[at] = jnp.where(sub == within, row, m[at])
    return jnp.concatenate(m, axis=0)


def fold(x):
    rows, width = x.shape
    x = jnp.sum(x.reshape(rows // 8, 8, width), axis=0)
    return functools.reduce(jnp.add, [x[:, n : n + 128] for n in range(0, width, 128)])


def kernel(
    rows,
    cols,
    row_tiles,
    col_tiles,
    range_length,
    smoothness,
    points_hbm,
    bank_hbm,
    ids_hbm,
    ranks_hbm,
    y_out,
    c_out,
    residuals,
    whole_out,
    ids,
    ranks,
    all_points,
    all_bank,
    low,
    norms,
    y_pair,
    w_pair,
    mine,
    sums,
    sem_local,
    sem_ps,
    sem_pr,
    sem_bs,
    sem_br,
    sem_sr,
    sem_ns,
    sem_nr,
    ready,
):
    p = lax.axis_index("prow")
    q = lax.axis_index("pcol")
    per_bank, sketch_rows, size = bank_hbm.shape
    slots = [(a, b) for a in range(row_tiles) for b in range(col_tiles)]
    sibling = q + 1 - 2 * lax.rem(q, 2)

    barrier = pltpu.get_barrier_semaphore()
    for step in range(1, cols):
        pl.semaphore_signal(
            barrier, device_id=(p, lax.rem(q + step, cols)), device_id_type=MESH
        )
    for step in range(1, rows):
        pl.semaphore_signal(
            barrier, device_id=(lax.rem(p + step, rows), q), device_id_type=MESH
        )
    own_bank = pl.ds(q * per_bank, per_bank)
    local = [
        pltpu.make_async_copy(source, target, sem_local.at[index])
        for index, (source, target) in enumerate(
            [
                (points_hbm.at[:, 0], all_points.at[q]),
                (bank_hbm, all_bank.at[own_bank]),
                (ids_hbm, ids),
                (ranks_hbm, ranks),
            ]
        )
    ]
    for copy in local:
        copy.start()
    needed = q < 0
    for a in range(row_tiles):
        needed = needed | (lax.rem(a * rows + p, cols) == q)
    y_pair[...] = jnp.zeros_like(y_pair)
    w_pair[...] = jnp.zeros_like(w_pair)
    for copy in local:
        copy.wait()
    pl.semaphore_wait(barrier, cols + rows - 2)
    for step in range(1, rows):
        pl.semaphore_signal(
            ready, device_id=(lax.rem(p + step, rows), q), device_id_type=MESH
        )

    def point_copy(source, target):
        return pltpu.make_async_remote_copy(
            src_ref=all_points.at[source],
            dst_ref=all_points.at[source],
            send_sem=sem_ps,
            recv_sem=sem_pr.at[source],
            device_id=(p, target),
            device_id_type=MESH,
        )

    def bank_copy(block, target, recv, count=1):
        at = pl.ds(block * per_bank, per_bank * count)
        return pltpu.make_async_remote_copy(
            src_ref=all_bank.at[at],
            dst_ref=all_bank.at[at],
            send_sem=sem_bs,
            recv_sem=recv,
            device_id=(p, target),
            device_id_type=MESH,
        )

    @pl.when(needed)
    def _():
        for step in range(1, cols):
            point_copy(q, lax.rem(q + step, cols)).start()

    for step in range(2, cols, 2):
        bank_copy(q, lax.rem(q + step, cols), sem_br.at[q]).start()
    bank_copy(q, sibling, sem_sr).start()

    degree = jnp.full((8, 128), smoothness[0].astype(F32))
    scale = (LOG2E * jnp.sqrt(2.0 * degree + 1.0)) / jnp.full((8, 128), range_length[0])
    scale = scale[:1]
    linear = jnp.where(smoothness[0] >= 1, 1.0 / LOG2E, 0.0).astype(F32)
    square = jnp.where(smoothness[0] >= 2, 1.0 / (3.0 * LOG2E * LOG2E), 0.0).astype(F32)

    def place(slot):
        a, b = slots[slot]
        return a * rows + p, b * cols + q

    arrived = []

    def generate(slot, begin=0, end=size // 128):
        i, j = place(slot)
        a = slots[slot][0]
        owner = lax.rem(a * rows + p, cols)
        fresh = owner != q
        for before in arrived:
            if before != a:
                fresh = fresh & (owner != lax.rem(before * rows + p, cols))
        if a not in arrived and begin == 0:
            arrived.append(a)

            @pl.when(fresh)
            def _():
                point_copy(owner, q).wait_recv()

        @pl.when(j > i)
        def _():
            norms[slot] = jnp.zeros((8, 128), F32)

            def clear(c, _):
                low[slot, pl.ds(pl.multiple_of(c * 128, 128), 128)] = jnp.zeros((128, size), BF16)
                return 0

            lax.fori_loop(begin, end, clear, 0)

        @pl.when(j <= i)
        def _():
            row_block = lax.rem(i, cols)
            row_major = i // cols
            col_major = slots[slot][1]

            def chunk(c, total):
                at = pl.ds(pl.multiple_of(c * 128, 128), 128)
                x_row = all_points[row_block, row_major, 0:1, at] * scale
                y_row = all_points[row_block, row_major, 1:2, at] * scale
                x_row = jnp.broadcast_to(x_row, (128, 128)).T
                y_row = jnp.broadcast_to(y_row, (128, 128)).T
                for n in range(size // 128):
                    cut = slice(n * 128, n * 128 + 128)
                    x_col = all_points[q, col_major, 0:1, cut] * scale
                    y_col = all_points[q, col_major, 1:2, cut] * scale
                    dx = x_row - x_col
                    dy = y_row - y_col
                    d2 = dx * dx + dy * dy
                    t = d2 * lax.rsqrt(jnp.maximum(d2, 1e-30))
                    tile = ((1.0 + linear * t + square * d2) * jnp.exp2(-t)).astype(BF16)
                    low[slot, at, cut] = tile
                    tile = tile.astype(F32)
                    total = total + jnp.sum((tile * tile).reshape(16, 8, 128), axis=0)
                return total

            total = jnp.zeros((8, 128), F32) if begin == 0 else norms[slot]
            norms[slot] = lax.fori_loop(begin, end, chunk, total)

    for slot in range(len(slots) - 1):
        generate(slot)
    split_at = size // 256
    generate(len(slots) - 1, 0, split_at)
    for step in range(2, cols, 2):
        block = lax.rem(q + step, cols)
        bank_copy(block, q, sem_br.at[block]).wait_recv()
        bank_copy(block, sibling, sem_sr).start()
    generate(len(slots) - 1, split_at)

    devices = rows * cols
    me = p * cols + q

    def norm_copy(target):
        return pltpu.make_async_remote_copy(
            src_ref=mine,
            dst_ref=sums.at[me],
            send_sem=sem_ns,
            recv_sem=sem_nr,
            device_id=(target // cols, lax.rem(target, cols)),
            device_id_type=MESH,
        )

    norm_sum = jnp.zeros((8, 128), F32)
    rank_sum = jnp.float32(0)
    for slot, (a, b) in enumerate(slots):
        i, j = place(slot)
        norm_sum = norm_sum + jnp.where(j < i, 2.0, 1.0).astype(F32) * norms[slot]
        rank_sum = rank_sum + jnp.where(j < i, ranks[0, b, 0, a], 0).astype(F32)
    mine[0:1, :] = jnp.sum(norm_sum, axis=0, keepdims=True)
    mine[1:2, :] = jnp.full((1, 128), rank_sum)
    sums[me] = mine[...]

    pl.semaphore_wait(ready, rows - 1)
    for step in range(1, devices):
        norm_copy(lax.rem(me + step, devices)).start()

    bank_copy(0, q, sem_sr, cols // 2).wait_recv()

    half = 64
    row_at = lax.broadcasted_iota(jnp.int32, (sketch_rows, 1), 0)

    def rank_of(slot):
        a, b = slots[slot]
        i, j = place(slot)
        return jnp.where(j < i, ranks[0, b, 0, a], 0)

    for first in range(0, len(slots), 2):
        pair = list(enumerate(range(first, min(first + 2, len(slots)))))
        products = []
        for side, slot in pair:
            a, b = slots[slot]
            sketch = all_bank[ids[0, b, 0, a]]
            sketch = jnp.where(row_at < rank_of(slot), sketch.astype(F32), 0.0).astype(BF16)
            y = dot(sketch, low[slot], 1, 1)
            y_out[a, 0, b, 0] = y
            y_pair[side * half : side * half + sketch_rows] = y
        for side, slot in pair:
            a, b = slots[slot]
            product = dot(jnp.concatenate(split(y_out[a, 0, b, 0]), axis=0), low[slot], 1, 0)
            w_pair[side * half : side * half + sketch_rows] = product[:sketch_rows]
            products.append(product[:sketch_rows] + 2.0 * product[sketch_rows:])
        gram = dot(y_pair[...], y_pair[...], 1, 1, HIGH)
        lane = lax.broadcasted_iota(jnp.int32, (sketch_rows, 2 * half), 1)
        sub = lax.broadcasted_iota(jnp.int32, (sketch_rows, 2 * half), 0)
        left = lane < half
        gram = jnp.where(left, gram[:sketch_rows], gram[half : half + sketch_rows])
        eye = lane == jnp.where(left, sub, sub + half)
        shifts = []
        diagonal = jnp.ones((sketch_rows, 2 * half), F32)
        for side, slot in pair:
            a, b = slots[slot]
            mask = left if side == 0 else ~left
            rank = jnp.full((1, 1), ranks[0, b, 0, a].astype(F32))
            shift = 0.1 * all_sum(jnp.where(eye & mask, gram, 0.0)) / rank
            shifts.append(shift)
            diagonal = jnp.where(mask & (sub < rank_of(slot)), shift, diagonal)
        inverse = invert(gram + jnp.where(eye, diagonal, 0.0), sketch_rows, half)
        inverse = jnp.concatenate(
            [jnp.where(left if side == 0 else ~left, inverse, 0.0) for side, _ in pair], axis=0
        )
        coefficients = dot(inverse, w_pair[...], 1, 0, HIGH)
        for side, slot in pair:
            a, b = slots[slot]
            i, j = place(slot)
            c = coefficients[side * sketch_rows : (side + 1) * sketch_rows]
            c_out[a, 0, b, 0] = c
            gain = fold(c * (products[side] + shifts[side] * c))
            residuals[slot] = norms[slot] - jnp.where(j < i, gain, 0.0)

    def norm_wait(ref):
        return pltpu.make_async_remote_copy(
            src_ref=ref,
            dst_ref=ref,
            send_sem=sem_ns,
            recv_sem=sem_nr,
            device_id=(p, sibling),
            device_id_type=MESH,
        )

    others = norm_wait(sums.at[pl.ds(0, devices - 1)])
    others.wait_recv()
    whole_out[...] = jnp.sum(sums[...], axis=0)
    others.wait_send()

    @pl.when(needed)
    def _():
        pltpu.make_async_remote_copy(
            src_ref=all_points.at[pl.ds(0, cols - 1)],
            dst_ref=all_points.at[pl.ds(0, cols - 1)],
            send_sem=sem_ps,
            recv_sem=sem_pr.at[0],
            device_id=(p, sibling),
            device_id_type=MESH,
        ).wait_send()

    bank_copy(0, sibling, sem_sr, cols - 1).wait_send()


def finish(rows, cols, row_tiles, col_tiles, y, c, residuals, whole, y_out, c_out, err_out, rank_out, sems):
    p = lax.axis_index("prow")
    q = lax.axis_index("pcol")
    copies = [
        pltpu.make_async_copy(source.at[a], target.at[a], sems.at[index, a])
        for index, (source, target) in enumerate([(y, y_out), (c, c_out)])
        for a in range(row_tiles)
    ]
    for copy in copies:
        copy.start()
    norm = lax.rsqrt(all_sum(whole[0:1, :])) * float(cols * col_tiles)
    lane = lax.broadcasted_iota(jnp.int32, (1, 128), 1)
    for b in range(col_tiles):
        line = jnp.zeros((1, 128), F32)
        for a in range(row_tiles):
            error = jnp.sqrt(jnp.maximum(all_sum(residuals[a * col_tiles + b]), 0.0)) * norm
            shown = (lane == a) & (b * cols + q <= a * rows + p)
            line = jnp.where(shown, error, line)
        err_out[0, b, 0:1, :] = line[:, :row_tiles]
    rank_out[0] = whole[1:2, 0:1].astype(jnp.int32)[0, 0]
    for copy in copies:
        copy.wait()


def per_device(rows, cols, points, range_length, smoothness, bank, ids, ranks):
    row_tiles, col_tiles = ids.shape[0], ids.shape[2]
    per_bank, sketch_rows, size = bank.shape
    slots = row_tiles * col_tiles
    ids = ids.transpose(1, 2, 3, 0)
    ranks = ranks.transpose(1, 2, 3, 0)
    factors = jax.ShapeDtypeStruct((row_tiles, 1, col_tiles, 1, sketch_rows, size), F32)
    vmem = pl.BlockSpec(memory_space=pltpu.VMEM)
    smem = pl.BlockSpec(memory_space=pltpu.SMEM)
    hbm = pl.BlockSpec(memory_space=pltpu.HBM)
    dma = pltpu.SemaphoreType.DMA
    pinned = [pltpu.with_memory_space_constraint(x, pltpu.HBM) for x in (points, bank, ids, ranks)]
    y, c, residuals, whole = pl.pallas_call(
        functools.partial(kernel, rows, cols, row_tiles, col_tiles),
        out_shape=(
            factors,
            factors,
            jax.ShapeDtypeStruct((slots, 8, 128), F32),
            jax.ShapeDtypeStruct((2, 128), F32),
        ),
        in_specs=[smem, smem, hbm, hbm, hbm, hbm],
        out_specs=(vmem,) * 4,
        scratch_shapes=[
            pltpu.SMEM(ids.shape, jnp.int32),
            pltpu.SMEM(ranks.shape, jnp.int32),
            pltpu.VMEM((cols, col_tiles, 2, size), F32),
            pltpu.VMEM((cols * per_bank, sketch_rows, size), BF16),
            pltpu.VMEM((slots, size, size), BF16),
            pltpu.VMEM((slots, 8, 128), F32),
            pltpu.VMEM((128, size), F32),
            pltpu.VMEM((128, size), F32),
            pltpu.VMEM((2, 128), F32),
            pltpu.VMEM((rows * cols, 2, 128), F32),
            dma((4,)),
            dma,
            dma((cols,)),
            dma,
            dma((cols,)),
            dma,
            dma,
            dma,
            pltpu.SemaphoreType.REGULAR,
        ],
        compiler_params=pltpu.CompilerParams(
            collective_id=0, has_side_effects=True, vmem_limit_bytes=40 * 1024 * 1024
        ),
        name="tiles",
    )(range_length, smoothness, *pinned)
    y, c, errors, rank_total = pl.pallas_call(
        functools.partial(finish, rows, cols, row_tiles, col_tiles),
        out_shape=(
            factors,
            factors,
            jax.ShapeDtypeStruct((1, col_tiles, 1, row_tiles), F32),
            jax.ShapeDtypeStruct((1,), jnp.int32),
        ),
        in_specs=[vmem] * 4,
        out_specs=(hbm, hbm, vmem, smem),
        scratch_shapes=[dma((2, row_tiles))],
        compiler_params=pltpu.CompilerParams(vmem_limit_bytes=16 * 1024 * 1024),
        name="finish",
    )(y, c, residuals, whole)
    return y, c, errors.transpose(3, 0, 1, 2), rank_total


def solution(mesh):
    in_specs = (
        P(None, "pcol", None, None),
        P(),
        P(),
        P("pcol", None, None),
        P(None, "prow", None, "pcol"),
        P(None, "prow", None, "pcol"),
    )
    out_specs = (
        P(None, "prow", None, "pcol", None, None),
        P(None, "prow", None, "pcol", None, None),
        P(None, "prow", None, "pcol"),
        P(),
    )
    return jax.shard_map(
        functools.partial(per_device, mesh.shape["prow"], mesh.shape["pcol"]),
        mesh=mesh,
        in_specs=in_specs,
        out_specs=out_specs,
        check_vma=False,
    )
```

time: 24 us -> 22.3 us (0.929)
  the two profiles are of different devices: /device:TPU:17 before, /device:TPU:0 now
where the time goes in v1:
time: 22.3 us; the launch traced here: 22.1 us
  Pallas kernels  20.2 us (91%)
  between operations  1.93 us (9%)
    pallas_call x1, Pallas kernels, per_device(): pl.pallas_call(functools.partial(kernel, rows, cols, row_tiles, col_tiles...  18.7 us
    pallas_call x1, Pallas kernels, per_device(): pl.pallas_call(functools.partial(finish, rows, cols, row_tiles, col_tiles...  1.43 us

profile of v1, /device:TPU:0, one launch (start us, length us, event | category | flops | bytes accessed | tf_op | source)
XLA Modules:
  0.0 22.1 jit_solution(13054293743913129492)
XLA Ops:
  1.9 18.7 %tiles.1 = (f32[2,1,1,1,48,1024]{5,4,3,2,1,0:T(8,128)S(1)}, f32[2,1,1,1,48,1024]{5,4,3,2,1,0:T(8,128)S(1)}, f32[2,8,128]{2,1,0:T(8,128)S(1)}, f32[2,128]{1,0:T(2,128)S(1)}) custom-call(f32[1]{0:T(128)S(6)} %copy.10.range_length, s32[1]{0:T(128)S(6)} %copy.11.smoothness, f32[1,1,2,1024]{3,2,1,0:T(2,128)} %points_hbm.1, bf16[1,48,1024]{2,1,0:T(8,128)(2,1)} %bank_hbm.1, ...), custom_call_target="tpu_custom_call" | custom-call | tf_op jit(solution)/shard_map/tiles/pallas_call | solution.py:397
  20.7 1.4 %finish.1 = (f32[2,1,1,1,48,1024]{5,4,3,2,1,0:T(8,128)}, f32[2,1,1,1,48,1024]{5,4,3,2,1,0:T(8,128)}, f32[1,1,1,2]{3,2,1,0:T(1,128)}, s32[1]{0:T(128)}) custom-call(f32[2,1,1,1,48,1024]{5,4,3,2,1,0:T(8,128)S(1)} %get-tuple-element.12.y, f32[2,1,1,1,48,1024]{5,4,3,2,1,0:T(8,128)S(1)} %get-tuple-element.13.c, f32[2,8,128]{2,1,0:T(8,128)S(1)} %get-tuple-element.14.residuals, ...), custom_call_target="tpu_custom_call" | custom-call | tf_op jit(solution)/shard_map/finish/pallas_call | solution.py:433

commit v2 on v1

--- a/solution.py
+++ b/solution.py
@@ -87,8 +87,9 @@
     all_bank,
     low,
     norms,
-    y_pair,
-    w_pair,
+    x_spread,
+    y_spread,
+    line,
     mine,
     sums,
     sem_local,
@@ -106,16 +107,25 @@
     per_bank, sketch_rows, size = bank_hbm.shape
     slots = [(a, b) for a in range(row_tiles) for b in range(col_tiles)]
     sibling = q + 1 - 2 * lax.rem(q, 2)
+    mirrored = row_tiles == 2 and col_tiles == 1 and cols == 2 * rows
 
     barrier = pltpu.get_barrier_semaphore()
     for step in range(1, cols):
         pl.semaphore_signal(
             barrier, device_id=(p, lax.rem(q + step, cols)), device_id_type=MESH
         )
-    for step in range(1, rows):
-        pl.semaphore_signal(
-            barrier, device_id=(lax.rem(p + step, rows), q), device_id_type=MESH
-        )
+    gate = q == 0
+
+    def tell_gates(semaphore):
+        for step in range(1, rows):
+            pl.semaphore_signal(
+                semaphore, device_id=(lax.rem(p + step, rows), 0), device_id_type=MESH
+            )
+
+    @pl.when(gate)
+    def _():
+        tell_gates(barrier)
+
     own_bank = pl.ds(q * per_bank, per_bank)
     local = [
         pltpu.make_async_copy(source, target, sem_local.at[index])
@@ -130,18 +140,46 @@
     ]
     for copy in local:
         copy.start()
-    needed = q < 0
-    for a in range(row_tiles):
-        needed = needed | (lax.rem(a * rows + p, cols) == q)
-    y_pair[...] = jnp.zeros_like(y_pair)
-    w_pair[...] = jnp.zeros_like(w_pair)
+    def place(slot):
+        a, b = slots[slot]
+        return a * rows + p, b * cols + q
+
+    def wants_bank(device):
+        wanted = device < 0
+        for a, b in slots:
+            wanted = wanted | (b * cols + device < a * rows + p)
+        return wanted
+
+    def wants_points(source, target):
+        if mirrored:
+            early = (source == p) & ((target < p) | (target >= p + rows))
+            return early | ((source == p + rows) & (target < source))
+        wanted = source < 0
+        for a in range(row_tiles):
+            wanted = wanted | (lax.rem(a * rows + p, cols) == source)
+        return wanted
+
+    bank_steps = []
+    for step in range(cols - 2, 0, -2):
+        other = lax.rem(q + step, cols)
+        twin = other + 1 - 2 * lax.rem(other, 2)
+        bank_steps.append((other, wants_bank(other) | wants_bank(twin)))
+    here, beside = wants_bank(q), wants_bank(sibling)
+
+    def clear(slot):
+        norms[slot] = jnp.zeros((8, 128), F32)
+
+        def chunk(c, _):
+            low[slot, pl.ds(pl.multiple_of(c * 128, 128), 128)] = jnp.zeros((128, size), BF16)
+            return 0
+
+        lax.fori_loop(0, size // 128, chunk, 0)
+
+    for slot in range(len(slots)):
+        i, j = place(slot)
+        pl.when(j > i)(functools.partial(clear, slot))
     for copy in local:
         copy.wait()
-    pl.semaphore_wait(barrier, cols + rows - 2)
-    for step in range(1, rows):
-        pl.semaphore_signal(
-            ready, device_id=(lax.rem(p + step, rows), q), device_id_type=MESH
-        )
 
     def point_copy(source, target):
         return pltpu.make_async_remote_copy(
@@ -164,90 +202,76 @@
             device_id_type=MESH,
         )
 
-    @pl.when(needed)
-    def _():
-        for step in range(1, cols):
-            point_copy(q, lax.rem(q + step, cols)).start()
-
-    for step in range(2, cols, 2):
-        bank_copy(q, lax.rem(q + step, cols), sem_br.at[q]).start()
-    bank_copy(q, sibling, sem_sr).start()
-
     degree = jnp.full((8, 128), smoothness[0].astype(F32))
     scale = (LOG2E * jnp.sqrt(2.0 * degree + 1.0)) / jnp.full((8, 128), range_length[0])
     scale = scale[:1]
-    linear = jnp.where(smoothness[0] >= 1, 1.0 / LOG2E, 0.0).astype(F32)
-    square = jnp.where(smoothness[0] >= 2, 1.0 / (3.0 * LOG2E * LOG2E), 0.0).astype(F32)
-
-    def place(slot):
-        a, b = slots[slot]
-        return a * rows + p, b * cols + q
-
-    arrived = []
+    linear, square = 1.0 / LOG2E, 1.0 / (3.0 * LOG2E * LOG2E)
+
+    def by_order(zero, one, two):
+        return jnp.where(smoothness[0] >= 2, two, jnp.where(smoothness[0] >= 1, one, zero)).astype(F32)
+
+    offset = by_order(-38.0, -31.0, math.log2(square))
+    first = by_order(0.0, linear * 2.0**31, linear / square)
+    constant = by_order(2.0**38, 2.0**31, 1.0 / square)
+    for b in range(col_tiles):
+        for n in range(0, size, 128):
+            cut = slice(n, n + 128)
+            x_own = all_points[q, b, 0:1, cut] * scale
+            y_own = all_points[q, b, 1:2, cut] * scale
+            x_spread[b, cut] = jnp.broadcast_to(x_own, (128, 128)).T
+            y_spread[b, cut] = jnp.broadcast_to(y_own, (128, 128)).T
 
     def generate(slot, begin=0, end=size // 128):
         i, j = place(slot)
-        a = slots[slot][0]
-        owner = lax.rem(a * rows + p, cols)
-        fresh = owner != q
-        for before in arrived:
-            if before != a:
-                fresh = fresh & (owner != lax.rem(before * rows + p, cols))
-        if a not in arrived and begin == 0:
-            arrived.append(a)
-
-            @pl.when(fresh)
-            def _():
-                point_copy(owner, q).wait_recv()
-
-        @pl.when(j > i)
-        def _():
-            norms[slot] = jnp.zeros((8, 128), F32)
-
-            def clear(c, _):
-                low[slot, pl.ds(pl.multiple_of(c * 128, 128), 128)] = jnp.zeros((128, size), BF16)
-                return 0
-
-            lax.fori_loop(begin, end, clear, 0)
-
-        @pl.when(j <= i)
-        def _():
-            row_block = lax.rem(i, cols)
-            row_major = i // cols
-            col_major = slots[slot][1]
-
-            def chunk(c, total):
-                at = pl.ds(pl.multiple_of(c * 128, 128), 128)
-                x_row = all_points[row_block, row_major, 0:1, at] * scale
-                y_row = all_points[row_block, row_major, 1:2, at] * scale
-                x_row = jnp.broadcast_to(x_row, (128, 128)).T
-                y_row = jnp.broadcast_to(y_row, (128, 128)).T
-                for n in range(size // 128):
-                    cut = slice(n * 128, n * 128 + 128)
-                    x_col = all_points[q, col_major, 0:1, cut] * scale
-                    y_col = all_points[q, col_major, 1:2, cut] * scale
-                    dx = x_row - x_col
-                    dy = y_row - y_col
-                    d2 = dx * dx + dy * dy
-                    t = d2 * lax.rsqrt(jnp.maximum(d2, 1e-30))
-                    tile = ((1.0 + linear * t + square * d2) * jnp.exp2(-t)).astype(BF16)
-                    low[slot, at, cut] = tile
-                    tile = tile.astype(F32)
-                    total = total + jnp.sum((tile * tile).reshape(16, 8, 128), axis=0)
-                return total
-
-            total = jnp.zeros((8, 128), F32) if begin == 0 else norms[slot]
-            norms[slot] = lax.fori_loop(begin, end, chunk, total)
-
-    for slot in range(len(slots) - 1):
-        generate(slot)
-    split_at = size // 256
-    generate(len(slots) - 1, 0, split_at)
-    for step in range(2, cols, 2):
-        block = lax.rem(q + step, cols)
-        bank_copy(block, q, sem_br.at[block]).wait_recv()
-        bank_copy(block, sibling, sem_sr).start()
-    generate(len(slots) - 1, split_at)
+        b = slots[slot][1]
+        row_block, row_major = lax.rem(i, cols), i // cols
+        for n in range(0, size, 128):
+            cut = slice(n, n + 128)
+            line[:, cut] = all_points[row_block, row_major, :, cut] * scale
+
+        def chunk(c, total):
+            at = pl.ds(pl.multiple_of(c * 128, 128), 128)
+            x_own, y_own = x_spread[b, at], y_spread[b, at]
+            for n in range(0, size, 128):
+                cut = slice(n, n + 128)
+                dx = x_own - line[0:1, cut]
+                dy = y_own - line[1:2, cut]
+                d2 = dx * dx + dy * dy
+                t = d2 * lax.rsqrt(jnp.maximum(d2, 1e-30))
+                tile = ((constant + t * (first + t)) * jnp.exp2(offset - t)).astype(BF16)
+                low[slot, at, cut] = tile
+                tile = tile.astype(F32)
+                total = total + jnp.sum((tile * tile).reshape(16, 8, 128), axis=0)
+            return total
+
+        total = jnp.zeros((8, 128), F32) if begin == 0 else norms[slot]
+        norms[slot] = lax.fori_loop(begin, end, chunk, total)
+
+    i, j = place(0)
+    pl.when((i == 0) & (j == 0))(functools.partial(generate, 0))
+
+    pl.semaphore_wait(barrier, cols - 1 + jnp.where(gate, rows - 1, 0))
+
+    point_targets = [lax.rem(q + cols - step, cols) for step in range(1, cols)]
+    for target in point_targets:
+        pl.when(wants_points(q, target))(point_copy(q, target).start)
+    for other, wanted in bank_steps:
+        pl.when(wanted)(bank_copy(q, other, sem_br.at[q]).start)
+    pl.when(beside)(bank_copy(q, sibling, sem_sr).start)
+    @pl.when(gate)
+    def _():
+        tell_gates(ready)
+
+    def open_gate():
+        pl.semaphore_wait(ready, rows - 1)
+        for step in range(1, cols):
+            pl.semaphore_signal(ready, device_id=(p, step), device_id_type=MESH)
+
+
+    def forward():
+        for other, _ in bank_steps:
+            pl.when(here | beside)(bank_copy(other, q, sem_br.at[other]).wait_recv)
+            pl.when(beside)(bank_copy(other, sibling, sem_sr).start)
 
     devices = rows * cols
     me = p * cols + q
@@ -262,21 +286,66 @@
             device_id_type=MESH,
         )
 
-    norm_sum = jnp.zeros((8, 128), F32)
-    rank_sum = jnp.float32(0)
-    for slot, (a, b) in enumerate(slots):
-        i, j = place(slot)
-        norm_sum = norm_sum + jnp.where(j < i, 2.0, 1.0).astype(F32) * norms[slot]
-        rank_sum = rank_sum + jnp.where(j < i, ranks[0, b, 0, a], 0).astype(F32)
-    mine[0:1, :] = jnp.sum(norm_sum, axis=0, keepdims=True)
-    mine[1:2, :] = jnp.full((1, 128), rank_sum)
-    sums[me] = mine[...]
-
-    pl.semaphore_wait(ready, rows - 1)
-    for step in range(1, devices):
-        norm_copy(lax.rem(me + step, devices)).start()
-
-    bank_copy(0, q, sem_sr, cols // 2).wait_recv()
+    def send_norms(weights):
+        norm_sum = jnp.zeros((8, 128), F32)
+        rank_sum = jnp.float32(0)
+        for slot, (a, b) in enumerate(slots):
+            i, j = place(slot)
+            norm_sum = norm_sum + weights[slot] * norms[slot]
+            rank_sum = rank_sum + jnp.where(j < i, ranks[0, b, 0, a], 0).astype(F32)
+        mine[0:1, :] = jnp.sum(norm_sum, axis=0, keepdims=True)
+        mine[1:2, :] = jnp.full((1, 128), rank_sum)
+        sums[me] = mine[...]
+        pl.when(~gate)(functools.partial(pl.semaphore_wait, ready, 1))
+        for step in range(1, devices):
+            norm_copy(lax.rem(me + step, devices)).start()
+
+    arrived = []
+
+    def await_points(a):
+        owner = lax.rem(a * rows + p, cols)
+        fresh = owner != q
+        for before in arrived:
+            fresh = fresh & (owner != lax.rem(before * rows + p, cols))
+        arrived.append(a)
+
+        @pl.when(fresh & wants_points(owner, q))
+        def _():
+            point_copy(owner, q).wait_recv()
+
+    if mirrored:
+        middle = size // 256
+        both, lone = q <= p, (q > p) & (q <= p + rows)
+        pl.when(q == p + rows)(functools.partial(generate, 1))
+        await_points(0)
+        pl.when(gate & (p > 0))(functools.partial(generate, 0, 0, middle))
+        pl.when(gate)(open_gate)
+        pl.when(gate & (p > 0))(functools.partial(generate, 0, middle))
+        pl.when((both & ~gate) | (q >= p + rows))(functools.partial(generate, 0))
+        await_points(1)
+        pl.when(lone & (q < p + rows))(functools.partial(generate, 1))
+        from_first = jnp.where((q < p) | (q >= p + rows), 2.0, jnp.where(q == p, 1.0, 0.0))
+        from_second = jnp.where(lone, jnp.where(q < p + rows, 2.0, 1.0), 0.0)
+        send_norms([from_first, from_second])
+        pl.when(both)(functools.partial(generate, 1, 0, middle))
+        pl.when(q == p)(functools.partial(generate, 1, middle))
+        forward()
+        pl.when(q < p)(functools.partial(generate, 1, middle))
+    else:
+        for slot, (a, b) in enumerate(slots):
+            i, j = place(slot)
+            if a not in arrived:
+                await_points(a)
+            pl.when((j <= i) & (i + j > 0) if slot == 0 else j <= i)(functools.partial(generate, slot))
+        pl.when(gate)(open_gate)
+        weights = []
+        for slot in range(len(slots)):
+            i, j = place(slot)
+            weights.append(jnp.where(j < i, 2.0, 1.0))
+        send_norms(weights)
+        forward()
+
+    pl.when(here)(bank_copy(0, q, sem_sr, cols // 2).wait_recv)
 
     half = 64
     row_at = lax.broadcasted_iota(jnp.int32, (sketch_rows, 1), 0)
@@ -286,22 +355,29 @@
         i, j = place(slot)
         return jnp.where(j < i, ranks[0, b, 0, a], 0)
 
+    blank = jnp.zeros((half - sketch_rows, size), BF16)
+
+    def stack(parts):
+        full = [x for part in parts for x in (part, blank)]
+        if len(parts) == 1:
+            full += full[:1] + [blank]
+        return jnp.concatenate(full, axis=0)
+
     for first in range(0, len(slots), 2):
         pair = list(enumerate(range(first, min(first + 2, len(slots)))))
-        products = []
+        highs, lows = [], []
         for side, slot in pair:
             a, b = slots[slot]
             sketch = all_bank[ids[0, b, 0, a]]
             sketch = jnp.where(row_at < rank_of(slot), sketch.astype(F32), 0.0).astype(BF16)
-            y = dot(sketch, low[slot], 1, 1)
+            y = dot(sketch, low[slot], 1, 0)
             y_out[a, 0, b, 0] = y
-            y_pair[side * half : side * half + sketch_rows] = y
-        for side, slot in pair:
-            a, b = slots[slot]
-            product = dot(jnp.concatenate(split(y_out[a, 0, b, 0]), axis=0), low[slot], 1, 0)
-            w_pair[side * half : side * half + sketch_rows] = product[:sketch_rows]
-            products.append(product[:sketch_rows] + 2.0 * product[sketch_rows:])
-        gram = dot(y_pair[...], y_pair[...], 1, 1, HIGH)
+            high, rest = split(y)
+            highs.append(high)
+            lows.append(rest)
+        high, rest = stack(highs), stack(lows)
+        gram = dot(jnp.concatenate([high, rest], axis=0), high, 1, 1)
+        gram = gram[: 2 * half] + gram[2 * half :] + dot(high, rest, 1, 1)
         lane = lax.broadcasted_iota(jnp.int32, (sketch_rows, 2 * half), 1)
         sub = lax.broadcasted_iota(jnp.int32, (sketch_rows, 2 * half), 0)
         left = lane < half
@@ -317,10 +393,20 @@
             shifts.append(shift)
             diagonal = jnp.where(mask & (sub < rank_of(slot)), shift, diagonal)
         inverse = invert(gram + jnp.where(eye, diagonal, 0.0), sketch_rows, half)
-        inverse = jnp.concatenate(
-            [jnp.where(left if side == 0 else ~left, inverse, 0.0) for side, _ in pair], axis=0
-        )
-        coefficients = dot(inverse, w_pair[...], 1, 0, HIGH)
+        products, highs_w, lows_w = [], [], []
+        for side, slot in pair:
+            product = dot(jnp.concatenate([highs[side], lows[side]], axis=0), low[slot], 1, 1)
+            high, rest = split(product[:sketch_rows])
+            highs_w.append(high)
+            lows_w.append(rest)
+            products.append(product[:sketch_rows] + 2.0 * product[sketch_rows:])
+        weights = jnp.concatenate([stack(highs_w), stack(lows_w)], axis=0)
+        sides = [jnp.where(left if side == 0 else ~left, inverse, 0.0) for side, _ in pair]
+        high, rest = split(jnp.concatenate(sides, axis=0))
+        terms = jnp.concatenate([high, rest], axis=0)
+        again = jnp.concatenate([high, jnp.zeros_like(rest)], axis=0)
+        terms = dot(jnp.concatenate([terms, again], axis=1), weights, 1, 0)
+        coefficients = terms[: len(pair) * sketch_rows] + terms[len(pair) * sketch_rows :]
         for side, slot in pair:
             a, b = slots[slot]
             i, j = place(slot)
@@ -344,18 +430,11 @@
     whole_out[...] = jnp.sum(sums[...], axis=0)
     others.wait_send()
 
-    @pl.when(needed)
-    def _():
-        pltpu.make_async_remote_copy(
-            src_ref=all_points.at[pl.ds(0, cols - 1)],
-            dst_ref=all_points.at[pl.ds(0, cols - 1)],
-            send_sem=sem_ps,
-            recv_sem=sem_pr.at[0],
-            device_id=(p, sibling),
-            device_id_type=MESH,
-        ).wait_send()
-
-    bank_copy(0, sibling, sem_sr, cols - 1).wait_send()
+    for target in point_targets:
+        pl.when(wants_points(q, target))(point_copy(q, target).wait_send)
+    for other, wanted in bank_steps:
+        pl.when(wanted)(bank_copy(q, other, sem_br.at[q]).wait_send)
+    pl.when(beside)(bank_copy(0, sibling, sem_sr, cols // 2).wait_send)
 
 
 def finish(rows, cols, row_tiles, col_tiles, y, c, residuals, whole, y_out, c_out, err_out, rank_out, sems):
@@ -411,8 +490,9 @@
             pltpu.VMEM((cols * per_bank, sketch_rows, size), BF16),
             pltpu.VMEM((slots, size, size), BF16),
             pltpu.VMEM((slots, 8, 128), F32),
-            pltpu.VMEM((128, size), F32),
-            pltpu.VMEM((128, size), F32),
+            pltpu.VMEM((col_tiles, size, 128), F32),
+            pltpu.VMEM((col_tiles, size, 128), F32),
+            pltpu.VMEM((2, size), F32),
             pltpu.VMEM((2, 128), F32),
             pltpu.VMEM((rows * cols, 2, 128), F32),
             dma((4,)),

time: 22.3 us -> 19.7 us (0.88)
  the two profiles are of different devices: /device:TPU:0 before, /device:TPU:1 now
where the time goes in v2:
time: 19.7 us; the launch traced here: 19.5 us
  Pallas kernels  17.5 us (89%)
  between operations  1.93 us (10%)
    pallas_call x1, Pallas kernels, per_device(): pl.pallas_call(functools.partial(kernel, rows, cols, row_tiles, col_tiles...  16.1 us
    pallas_call x1, Pallas kernels, per_device(): pl.pallas_call(functools.partial(finish, rows, cols, row_tiles, col_tiles...  1.43 us

profile of v2, /device:TPU:1, one launch (start us, length us, event | category | flops | bytes accessed | tf_op | source)
XLA Modules:
  0.0 19.5 jit_solution(8401931124624868510)
XLA Ops:
  1.9 16.1 %tiles.1 = (f32[2,1,1,1,48,1024]{5,4,3,2,1,0:T(8,128)S(1)}, f32[2,1,1,1,48,1024]{5,4,3,2,1,0:T(8,128)S(1)}, f32[2,8,128]{2,1,0:T(8,128)S(1)}, f32[2,128]{1,0:T(2,128)S(1)}) custom-call(f32[1]{0:T(128)S(6)} %copy.10.range_length, s32[1]{0:T(128)S(6)} %copy.11.smoothness, f32[1,1,2,1024]{3,2,1,0:T(2,128)} %points_hbm.1, bf16[1,48,1024]{2,1,0:T(8,128)(2,1)} %bank_hbm.1, ...), custom_call_target="tpu_custom_call" | custom-call | tf_op jit(solution)/shard_map/tiles/pallas_call | solution.py:476
  18.0 1.4 %finish.1 = (f32[2,1,1,1,48,1024]{5,4,3,2,1,0:T(8,128)}, f32[2,1,1,1,48,1024]{5,4,3,2,1,0:T(8,128)}, f32[1,1,1,2]{3,2,1,0:T(1,128)}, s32[1]{0:T(128)}) custom-call(f32[2,1,1,1,48,1024]{5,4,3,2,1,0:T(8,128)S(1)} %get-tuple-element.12.y, f32[2,1,1,1,48,1024]{5,4,3,2,1,0:T(8,128)S(1)} %get-tuple-element.13.c, f32[2,8,128]{2,1,0:T(8,128)S(1)} %get-tuple-element.14.residuals, ...), custom_call_target="tpu_custom_call" | custom-call | tf_op jit(solution)/shard_map/finish/pallas_call | solution.py:513

commit v3 on v2

--- a/solution.py
+++ b/solution.py
@@ -160,7 +160,7 @@
         return wanted
 
     bank_steps = []
-    for step in range(cols - 2, 0, -2):
+    for step in sorted(range(2, cols, 2), key=lambda step: step == cols // 2):
         other = lax.rem(q + step, cols)
         twin = other + 1 - 2 * lax.rem(other, 2)
         bank_steps.append((other, wants_bank(other) | wants_bank(twin)))
@@ -178,6 +178,11 @@
     for slot in range(len(slots)):
         i, j = place(slot)
         pl.when(j > i)(functools.partial(clear, slot))
+
+        @pl.when(j >= i)
+        def _():
+            a, b = slots[slot]
+            y_out[a, 0, b, 0] = jnp.zeros((sketch_rows, size), F32)
     for copy in local:
         copy.wait()
 
@@ -255,7 +260,9 @@
     point_targets = [lax.rem(q + cols - step, cols) for step in range(1, cols)]
     for target in point_targets:
         pl.when(wants_points(q, target))(point_copy(q, target).start)
-    for other, wanted in bank_steps:
+    for other, wanted in bank_steps[:-1]:
+        pl.when(wanted)(bank_copy(q, other, sem_br.at[q]).start)
+    for other, wanted in bank_steps[-1:]:
         pl.when(wanted)(bank_copy(q, other, sem_br.at[q]).start)
     pl.when(beside)(bank_copy(q, sibling, sem_sr).start)
     @pl.when(gate)
@@ -323,14 +330,18 @@
         pl.when(gate & (p > 0))(functools.partial(generate, 0, middle))
         pl.when((both & ~gate) | (q >= p + rows))(functools.partial(generate, 0))
         await_points(1)
-        pl.when(lone & (q < p + rows))(functools.partial(generate, 1))
+        alone = lone & (q < p + rows)
+        early = alone & (sibling == p)
+        late = size * 3 // 512
+        pl.when(alone)(functools.partial(generate, 1, 0, late))
+        pl.when(early)(forward)
+        pl.when(alone)(functools.partial(generate, 1, late))
         from_first = jnp.where((q < p) | (q >= p + rows), 2.0, jnp.where(q == p, 1.0, 0.0))
         from_second = jnp.where(lone, jnp.where(q < p + rows, 2.0, 1.0), 0.0)
         send_norms([from_first, from_second])
         pl.when(both)(functools.partial(generate, 1, 0, middle))
-        pl.when(q == p)(functools.partial(generate, 1, middle))
-        forward()
-        pl.when(q < p)(functools.partial(generate, 1, middle))
+        pl.when(~early)(forward)
+        pl.when(both)(functools.partial(generate, 1, middle))
     else:
         for slot, (a, b) in enumerate(slots):
             i, j = place(slot)
@@ -355,6 +366,16 @@
         i, j = place(slot)
         return jnp.where(j < i, ranks[0, b, 0, a], 0)
 
+    def valid(slot):
+        i, j = place(slot)
+        return j < i
+
+    def sketch_tile(slot):
+        a, b = slots[slot]
+        sketch = all_bank[ids[0, b, 0, a]]
+        sketch = jnp.where(row_at < ranks[0, b, 0, a], sketch.astype(F32), 0.0).astype(BF16)
+        y_out[a, 0, b, 0] = dot(sketch, low[slot], 1, 0)
+
     blank = jnp.zeros((half - sketch_rows, size), BF16)
 
     def stack(parts):
@@ -367,12 +388,10 @@
         pair = list(enumerate(range(first, min(first + 2, len(slots)))))
         highs, lows = [], []
         for side, slot in pair:
+            pl.when(valid(slot))(functools.partial(sketch_tile, slot))
+        for side, slot in pair:
             a, b = slots[slot]
-            sketch = all_bank[ids[0, b, 0, a]]
-            sketch = jnp.where(row_at < rank_of(slot), sketch.astype(F32), 0.0).astype(BF16)
-            y = dot(sketch, low[slot], 1, 0)
-            y_out[a, 0, b, 0] = y
-            high, rest = split(y)
+            high, rest = split(y_out[a, 0, b, 0])
             highs.append(high)
             lows.append(rest)
         high, rest = stack(highs), stack(lows)
@@ -430,8 +449,15 @@
     whole_out[...] = jnp.sum(sums[...], axis=0)
     others.wait_send()
 
-    for target in point_targets:
-        pl.when(wants_points(q, target))(point_copy(q, target).wait_send)
+    owns_points = q < 0
+    for a in range(row_tiles):
+        owns_points = owns_points | (lax.rem(a * rows + p, cols) == q)
+
+    @pl.when(owns_points)
+    def _():
+        for target in point_targets:
+            pl.when(wants_points(q, target))(point_copy(q, target).wait_send)
+
     for other, wanted in bank_steps:
         pl.when(wanted)(bank_copy(q, other, sem_br.at[q]).wait_send)
     pl.when(beside)(bank_copy(0, sibling, sem_sr, cols // 2).wait_send)

time: 19.7 us -> 18.8 us (0.954)
  the two profiles are of different devices: /device:TPU:1 before, /device:TPU:0 now
where the time goes in v3:
time: 18.8 us; the launch traced here: 18.6 us
  Pallas kernels  16.6 us (88%)
  between operations  1.93 us (10%)
    pallas_call x1, Pallas kernels, per_device(): pl.pallas_call(functools.partial(kernel, rows, cols, row_tiles, col_tiles...  15.2 us
    pallas_call x1, Pallas kernels, per_device(): pl.pallas_call(functools.partial(finish, rows, cols, row_tiles, col_tiles...  1.43 us

profile of v3, /device:TPU:0, one launch (start us, length us, event | category | flops | bytes accessed | tf_op | source)
XLA Modules:
  0.0 18.6 jit_solution(291950254513436243)
XLA Ops:
  1.9 15.2 %tiles.1 = (f32[2,1,1,1,48,1024]{5,4,3,2,1,0:T(8,128)S(1)}, f32[2,1,1,1,48,1024]{5,4,3,2,1,0:T(8,128)S(1)}, f32[2,8,128]{2,1,0:T(8,128)S(1)}, f32[2,128]{1,0:T(2,128)S(1)}) custom-call(f32[1]{0:T(128)S(6)} %copy.10.range_length, s32[1]{0:T(128)S(6)} %copy.11.smoothness, f32[1,1,2,1024]{3,2,1,0:T(2,128)} %points_hbm.1, bf16[1,48,1024]{2,1,0:T(8,128)(2,1)} %bank_hbm.1, ...), custom_call_target="tpu_custom_call" | custom-call | tf_op jit(solution)/shard_map/tiles/pallas_call | solution.py:502
  17.1 1.4 %finish.1 = (f32[2,1,1,1,48,1024]{5,4,3,2,1,0:T(8,128)}, f32[2,1,1,1,48,1024]{5,4,3,2,1,0:T(8,128)}, f32[1,1,1,2]{3,2,1,0:T(1,128)}, s32[1]{0:T(128)}) custom-call(f32[2,1,1,1,48,1024]{5,4,3,2,1,0:T(8,128)S(1)} %get-tuple-element.12.y, f32[2,1,1,1,48,1024]{5,4,3,2,1,0:T(8,128)S(1)} %get-tuple-element.13.c, f32[2,8,128]{2,1,0:T(8,128)S(1)} %get-tuple-element.14.residuals, ...), custom_call_target="tpu_custom_call" | custom-call | tf_op jit(solution)/shard_map/finish/pallas_call | solution.py:539

commit v4 on v3

--- a/solution.py
+++ b/solution.py
@@ -160,8 +160,10 @@
         return wanted
 
     bank_steps = []
-    for step in sorted(range(2, cols, 2), key=lambda step: step == cols // 2):
-        other = lax.rem(q + step, cols)
+    turned = q + 2 - 4 * lax.rem(q // 2, 2)
+    nearest = [turned] + [lax.rem(q + step, cols) for step in range(4, cols, 4)]
+    farther = [lax.rem(turned + step, cols) for step in range(4, cols, 4)]
+    for other in nearest + farther:
         twin = other + 1 - 2 * lax.rem(other, 2)
         bank_steps.append((other, wants_bank(other) | wants_bank(twin)))
     here, beside = wants_bank(q), wants_bank(sibling)
@@ -260,9 +262,10 @@
     point_targets = [lax.rem(q + cols - step, cols) for step in range(1, cols)]
     for target in point_targets:
         pl.when(wants_points(q, target))(point_copy(q, target).start)
-    for other, wanted in bank_steps[:-1]:
+    for other, wanted in bank_steps[: len(nearest)]:
         pl.when(wanted)(bank_copy(q, other, sem_br.at[q]).start)
-    for other, wanted in bank_steps[-1:]:
+    pl.when((q != p) & (q != p + rows))(lambda: pl.delay(800))
+    for other, wanted in bank_steps[len(nearest) :]:
         pl.when(wanted)(bank_copy(q, other, sem_br.at[q]).start)
     pl.when(beside)(bank_copy(q, sibling, sem_sr).start)
     @pl.when(gate)
@@ -309,14 +312,16 @@
 
     arrived = []
 
-    def await_points(a):
+    def await_points(a, skip=None):
         owner = lax.rem(a * rows + p, cols)
         fresh = owner != q
         for before in arrived:
             fresh = fresh & (owner != lax.rem(before * rows + p, cols))
         arrived.append(a)
 
-        @pl.when(fresh & wants_points(owner, q))
+        fresh = fresh & wants_points(owner, q)
+
+        @pl.when(fresh if skip is None else fresh & ~skip)
         def _():
             point_copy(owner, q).wait_recv()
 
@@ -325,11 +330,14 @@
         both, lone = q <= p, (q > p) & (q <= p + rows)
         pl.when(q == p + rows)(functools.partial(generate, 1))
         await_points(0)
+        corner = gate & (p == 0)
+        pl.when(corner)(point_copy(rows, q).wait_recv)
+        pl.when(corner)(functools.partial(generate, 1, 0, middle))
         pl.when(gate & (p > 0))(functools.partial(generate, 0, 0, middle))
         pl.when(gate)(open_gate)
         pl.when(gate & (p > 0))(functools.partial(generate, 0, middle))
         pl.when((both & ~gate) | (q >= p + rows))(functools.partial(generate, 0))
-        await_points(1)
+        await_points(1, corner)
         alone = lone & (q < p + rows)
         early = alone & (sibling == p)
         late = size * 3 // 512
@@ -339,7 +347,7 @@
         from_first = jnp.where((q < p) | (q >= p + rows), 2.0, jnp.where(q == p, 1.0, 0.0))
         from_second = jnp.where(lone, jnp.where(q < p + rows, 2.0, 1.0), 0.0)
         send_norms([from_first, from_second])
-        pl.when(both)(functools.partial(generate, 1, 0, middle))
+        pl.when(both & ~corner)(functools.partial(generate, 1, 0, middle))
         pl.when(~early)(forward)
         pl.when(both)(functools.partial(generate, 1, middle))
     else:
@@ -387,8 +395,17 @@
     for first in range(0, len(slots), 2):
         pair = list(enumerate(range(first, min(first + 2, len(slots)))))
         highs, lows = [], []
-        for side, slot in pair:
-            pl.when(valid(slot))(functools.partial(sketch_tile, slot))
+        wanted = [valid(slot) for _, slot in pair]
+        every = functools.reduce(jnp.logical_and, wanted)
+
+        @pl.when(every)
+        def _():
+            for _, slot in pair:
+                sketch_tile(slot)
+
+        for (_, slot), want in zip(pair, wanted):
+            pl.when(want & ~every)(functools.partial(sketch_tile, slot))
+
         for side, slot in pair:
             a, b = slots[slot]
             high, rest = split(y_out[a, 0, b, 0])

time: 18.8 us -> 18.5 us (0.984)
  Pallas kernels: 16.6 us -> 16.4 us
    pallas_call x1, Pallas kernels: 15.2 us -> 14.9 us  [per_device(): pl.pallas_call(functools.partial(kernel, rows, cols, row_tiles, col_tiles...]
where the time goes in v4:
time: 18.5 us; the launch traced here: 18.3 us
  Pallas kernels  16.4 us (89%)
  between operations  1.93 us (10%)
    pallas_call x1, Pallas kernels, per_device(): pl.pallas_call(functools.partial(kernel, rows, cols, row_tiles, col_tiles...  14.9 us
    pallas_call x1, Pallas kernels, per_device(): pl.pallas_call(functools.partial(finish, rows, cols, row_tiles, col_tiles...  1.43 us

profile of v4, /device:TPU:0, one launch (start us, length us, event | category | flops | bytes accessed | tf_op | source)
XLA Modules:
  0.0 18.3 jit_solution(4690545183729331094)
XLA Ops:
  1.9 14.9 %tiles.1 = (f32[2,1,1,1,48,1024]{5,4,3,2,1,0:T(8,128)S(1)}, f32[2,1,1,1,48,1024]{5,4,3,2,1,0:T(8,128)S(1)}, f32[2,8,128]{2,1,0:T(8,128)S(1)}, f32[2,128]{1,0:T(2,128)S(1)}) custom-call(f32[1]{0:T(128)S(6)} %copy.10.range_length, s32[1]{0:T(128)S(6)} %copy.11.smoothness, f32[1,1,2,1024]{3,2,1,0:T(2,128)} %points_hbm.1, bf16[1,48,1024]{2,1,0:T(8,128)(2,1)} %bank_hbm.1, ...), custom_call_target="tpu_custom_call" | custom-call | tf_op jit(solution)/shard_map/tiles/pallas_call | solution.py:519
  16.9 1.4 %finish.1 = (f32[2,1,1,1,48,1024]{5,4,3,2,1,0:T(8,128)}, f32[2,1,1,1,48,1024]{5,4,3,2,1,0:T(8,128)}, f32[1,1,1,2]{3,2,1,0:T(1,128)}, s32[1]{0:T(128)}) custom-call(f32[2,1,1,1,48,1024]{5,4,3,2,1,0:T(8,128)S(1)} %get-tuple-element.12.y, f32[2,1,1,1,48,1024]{5,4,3,2,1,0:T(8,128)S(1)} %get-tuple-element.13.c, f32[2,8,128]{2,1,0:T(8,128)S(1)} %get-tuple-element.14.residuals, ...), custom_call_target="tpu_custom_call" | custom-call | tf_op jit(solution)/shard_map/finish/pallas_call | solution.py:556

commit v5 on v4

--- a/solution.py
+++ b/solution.py
@@ -347,9 +347,11 @@
         from_first = jnp.where((q < p) | (q >= p + rows), 2.0, jnp.where(q == p, 1.0, 0.0))
         from_second = jnp.where(lone, jnp.where(q < p + rows, 2.0, 1.0), 0.0)
         send_norms([from_first, from_second])
-        pl.when(both & ~corner)(functools.partial(generate, 1, 0, middle))
+        quarter = size // 512
+        pl.when(both & ~corner)(functools.partial(generate, 1, 0, quarter))
         pl.when(~early)(forward)
-        pl.when(both)(functools.partial(generate, 1, middle))
+        pl.when(both & ~corner)(functools.partial(generate, 1, quarter))
+        pl.when(corner)(functools.partial(generate, 1, middle))
     else:
         for slot, (a, b) in enumerate(slots):
             i, j = place(slot)

time: 18.5 us -> 18.5 us (level)
  no operation moved by 1% of the time
where the time goes in v5:
time: 18.5 us; the launch traced here: 18.3 us
  Pallas kernels  16.4 us (89%)
  between operations  1.93 us (10%)
    pallas_call x1, Pallas kernels, per_device(): pl.pallas_call(functools.partial(kernel, rows, cols, row_tiles, col_tiles...  14.9 us
    pallas_call x1, Pallas kernels, per_device(): pl.pallas_call(functools.partial(finish, rows, cols, row_tiles, col_tiles...  1.43 us

profile of v5, /device:TPU:0, one launch (start us, length us, event | category | flops | bytes accessed | tf_op | source)
XLA Modules:
  0.0 18.3 jit_solution(4436602928258336234)
XLA Ops:
  1.9 14.9 %tiles.1 = (f32[2,1,1,1,48,1024]{5,4,3,2,1,0:T(8,128)S(1)}, f32[2,1,1,1,48,1024]{5,4,3,2,1,0:T(8,128)S(1)}, f32[2,8,128]{2,1,0:T(8,128)S(1)}, f32[2,128]{1,0:T(2,128)S(1)}) custom-call(f32[1]{0:T(128)S(6)} %copy.10.range_length, s32[1]{0:T(128)S(6)} %copy.11.smoothness, f32[1,1,2,1024]{3,2,1,0:T(2,128)} %points_hbm.1, bf16[1,48,1024]{2,1,0:T(8,128)(2,1)} %bank_hbm.1, ...), custom_call_target="tpu_custom_call" | custom-call | tf_op jit(solution)/shard_map/tiles/pallas_call | solution.py:521
  16.9 1.4 %finish.1 = (f32[2,1,1,1,48,1024]{5,4,3,2,1,0:T(8,128)}, f32[2,1,1,1,48,1024]{5,4,3,2,1,0:T(8,128)}, f32[1,1,1,2]{3,2,1,0:T(1,128)}, s32[1]{0:T(128)}) custom-call(f32[2,1,1,1,48,1024]{5,4,3,2,1,0:T(8,128)S(1)} %get-tuple-element.12.y, f32[2,1,1,1,48,1024]{5,4,3,2,1,0:T(8,128)S(1)} %get-tuple-element.13.c, f32[2,8,128]{2,1,0:T(8,128)S(1)} %get-tuple-element.14.residuals, ...), custom_call_target="tpu_custom_call" | custom-call | tf_op jit(solution)/shard_map/finish/pallas_call | solution.py:558
